TPU v7x, 128 devices: a whole 4x4x4 slice. The times are simulated.
128 devices in a mesh: dp: 8 (over x, core), tensor: 16 (over y, z).
Axes of the slice: x: 4, y: 4, z: 4, core: 2. Of those that a mesh axis runs over, the one named last changes fastest.
Arguments:
- hidden: bfloat16 [16, 64, 4608], P('dp', 'tensor'), may hold values from -6 to 6
- gain: float32 [4608], replicated, may hold values from 0.5 to 1.5
- labels: int32 [16, 64], P('dp', 'tensor'), may hold values from 0 to 255999
- lengths: int32 [16], replicated, may hold values from 1 to 64
- embed: bfloat16 [256000, 4608], P(('dp', 'tensor')), may hold values from -0.375 to 0.375
Outputs:
- token_logprob: float32 [16, 64], P('dp', 'tensor')
- mean_nll: float32 [], replicated
- z_loss: float32 [], replicated
All inputs are finite; a program needn't handle non-finite values.
Results may differ from a plain program's by a relative error of at most 0.00058.
Values may be sent and summed in bfloat16 or wider, within the bound.
No kernel may reach another device: no remote copies, remote signals or barrier semaphores. Data moves between devices by JAX's collectives and lax.ppermute only.
A program may use at most 128 MiB of HBM per device.

v0:
```python
import jax
import jax.numpy as jnp
from jax import lax
from jax.sharding import Mesh
from jax.sharding import PartitionSpec as P

CAP = 30
TENSOR = ("tensor_0", "tensor_1")
DP = ("dp_0", "dp_1")
DP_TENSOR = ("dp_0", "dp_1", "tensor_0", "tensor_1")


def joined_along(pieces, dim):
    lengths = list(pieces.shape[1:])
    lengths[dim] *= pieces.shape[0]
    return jnp.moveaxis(pieces, 0, dim).reshape(lengths)


def gather_in_order(value, axes, order):
    pieces = value[None]
    for k in order:
        pieces = lax.all_gather(pieces, axes[k], axis=0, tiled=True)
    block = [lax.axis_size(axes[k]) for k in reversed(order)]
    pieces = pieces.reshape(*block, *value.shape)
    turned = sorted(range(len(order)), key=lambda place: order[len(order) - 1 - place])
    return pieces.transpose(*turned, *range(len(order), pieces.ndim)).reshape(-1, *value.shape)


def gathered_by_axis(value, axes, order, dim):
    return joined_along(gather_in_order(value, axes, order), dim)


def one_axis_at_a_time(value, axes):
    for axis in axes:
        value = lax.psum(value, axis)
    return value


def normalize(rows, gain):
    values = rows.astype(jnp.float32)
    meansq = jnp.mean(values * values, axis=-1, keepdims=True)
    return (values * lax.rsqrt(meansq + 1e-06) * gain).astype(jnp.bfloat16)


def per_device(hidden, gain, labels, lengths, embed):
    n_tensor = lax.axis_size(TENSOR)
    n_all = lax.axis_size(DP) * n_tensor
    seqs, stretch, width = hidden.shape
    vocab_dev = embed.shape[0]
    rows_local = seqs * stretch
    total_rows = rows_local * n_all
    flat = hidden.reshape(rows_local, width)
    row_ids = jnp.arange(total_rows)
    owner = row_ids // rows_local
    within = row_ids % rows_local
    batch_ids = owner // n_tensor * seqs + within // stretch
    positions = owner % n_tensor * stretch + within % stretch
    live_all = (positions < jnp.take(lengths, batch_ids)).astype(jnp.float32)
    all_labels = gathered_by_axis(labels.reshape(rows_local), DP_TENSOR, (0, 2, 3, 1), 0)
    rows = normalize(lax.all_gather(flat, DP_TENSOR, axis=0, tiled=True), gain)
    values = lax.dot_general(
        rows, embed, (((1,), (1,)), ((), ())), preferred_element_type=jnp.float32
    )
    capped = CAP * jnp.tanh(values / CAP)
    sumexp = jnp.sum(jnp.exp(capped), axis=1)
    first = lax.axis_index(DP_TENSOR) * vocab_dev
    local = all_labels - first
    inside = (local >= 0) & (local < vocab_dev)
    chosen = jnp.take_along_axis(capped, jnp.clip(local, 0, vocab_dev - 1)[:, None], axis=1)[:, 0]
    picked = jnp.where(inside, chosen, jnp.float32(0.0))
    own_start = lax.axis_index(DP_TENSOR) * rows_local
    sum_total, pick_total = (
        one_axis_at_a_time(sumexp, DP_TENSOR),
        one_axis_at_a_time(picked, DP_TENSOR),
    )
    own_sum = lax.dynamic_slice_in_dim(sum_total, own_start, rows_local)
    own_pick = lax.dynamic_slice_in_dim(pick_total, own_start, rows_local)
    own_live = lax.dynamic_slice_in_dim(live_all, own_start, rows_local)
    lse = jnp.log(own_sum)
    token = own_live * (own_pick - lse)
    nll_sum, count, square_sum = (
        one_axis_at_a_time(-jnp.sum(token), DP_TENSOR),
        one_axis_at_a_time(jnp.sum(own_live), DP_TENSOR),
        one_axis_at_a_time(jnp.sum(own_live * lse * lse), DP_TENSOR),
    )
    mean_nll = nll_sum / count
    z_loss = 0.01 * square_sum / count
    return (token.reshape(seqs, stretch), mean_nll, z_loss)


def solution(mesh):
    finer = Mesh(mesh.devices.reshape(4, 2, 4, 4), ("dp_0", "dp_1", "tensor_0", "tensor_1"))
    placed = (P(DP, TENSOR, None), P(), P(DP, TENSOR), P(), P(DP_TENSOR, None))
    return jax.shard_map(
        per_device,
        mesh=finer,
        in_specs=placed,
        out_specs=(P(DP, TENSOR), P(), P()),
        check_vma=False,
    )
```

profile of v0, /device:TPU:0, one launch (start us, length us, event | category | flops | bytes accessed | tf_op | source)
XLA Modules:
  0.0 235.7 jit_solution(905636388065802860)
XLA Ops:
  7.2 0.0 copy-start.1
  7.2 0.0 all-gather.6.cloned.1.call-start
  7.2 1.5 reshape.258
  8.8 0.0 all-gather.6.cloned.1.call-update
  8.8 0.8 reshape.330
  9.5 9.8 %all-gather = s32[4,1,8]{2,1,0:T(1,128)S(1)} all-gather(s32[1,1,8]{2,1,0:T(1,128)S(1)} %reshape.330), channel_id=1, replica_groups=mesh['dp_0'=4,'dp_1'=2,'tensor_0'=4,'tensor_1'=4] {'dp_0'}, dimensions={0}, use_global_device_ids=true | all-gather | bytes 160 | tf_op jit(solution)/shard_map/all_gather | solution.py:22
  19.4 11.3 %all-gather.1 = s32[4,4,8]{2,1,0:T(4,128)S(1)} all-gather(s32[1,4,8]{2,1,0:T(4,128)S(1)} %bitcast.36), channel_id=1, replica_groups=mesh['dp_0'=4,'dp_1'=2,'tensor_0'=4,'tensor_1'=4] {'tensor_0'}, dimensions={0}, use_global_device_ids=true | all-gather | bytes 640 | tf_op jit(solution)/shard_map/all_gather | solution.py:22
  30.7 0.1 copy.22
  30.8 13.2 %all-gather.2 = s32[4,16,8]{1,2,0:T(8,128)S(1)} all-gather(s32[1,16,8]{1,2,0:T(8,128)S(1)} %copy.22), channel_id=1, replica_groups=mesh['dp_0'=4,'dp_1'=2,'tensor_0'=4,'tensor_1'=4] {'tensor_1'}, dimensions={0}, use_global_device_ids=true | all-gather | bytes 2560 | tf_op jit(solution)/shard_map/all_gather | solution.py:22
  44.0 0.1 reshape.336
  44.1 1.8 all-gather.3
  45.9 0.1 copy.26
  46.0 0.1 min.24
  46.1 0.1 min.22
  46.2 0.1 copy.24
  46.4 0.1 and.146
  46.5 0.1 compare_reduce_fusion
  46.6 0.1 compare_reduce_fusion.1
  46.6 0.1 compare_reduce_fusion.2
  46.7 0.1 compare_reduce_fusion.3
  46.7 0.1 compare_reduce_fusion.4
  46.8 0.1 compare_reduce_fusion.5
  46.8 0.1 compare_reduce_fusion.6
  46.9 0.1 compare_reduce_fusion.7
  47.0 0.1 compare_reduce_fusion.8
  47.0 2.0 fusion.37
  49.0 4.4 %compare_select_fusion.2 = s32[1024,1]{0,1:T(1,128)S(1)} fusion(s32[]{:T(128)} %bitcast.9, s32[]{:T(128)} %bitcast.10, s32[]{:T(128)} %bitcast.11, s32[]{:T(128)} %bitcast.12, s32[]{:T(128)} %bitcast.13, s32[]{:T(128)} %bitcast.15, s32[]{:T(128)} %bitcast.14), kind=kLoop, calls=%fused_computation.22 | loop fusion | flops 60416 | bytes 4124 | tf_op jit(solution)/shard_map/jit(_take)/gather | solution.py:58
  53.5 5.8 %fusion.34 = f32[1024]{0:T(1024)S(1)} fusion(pred[1024]{0:T(1024)(128)(4,1)S(1)} %compare_reduce_fusion, pred[1024]{0:T(1024)(128)(4,1)S(1)} %compare_reduce_fusion.1, pred[1024]{0:T(1024)(128)(4,1)S(1)} %compare_reduce_fusion.2, pred[1024]{0:T(1024)(128)(4,1)S(1)} %compare_reduce_fusion.3, pred[1024]{0:T(1024)(128)(4,1)S(1)} %compare_reduce_fusion.4, ...), kind=kLoop, calls=%fused_computation.90 | loop fusion | flops 73728 | bytes 17444 | tf_op jit(solution)/shard_map/convert_element_type | solution.py:58
  59.3 24.7 %all-gather.6.cloned.1.call-done = bf16[1024,4608]{1,0:T(8,128)(2,1)} async-done(((bf16[8,4608]{1,0:T(8,128)(2,1)}), bf16[1024,4608]{1,0:T(8,128)(2,1)}) %all-gather.6.cloned.1.call-update) | async-done | bytes 9437200 | tf_op jit(solution)/shard_map/all_gather | solution.py:60
  84.0 0.0 copy-start
  84.0 5.7 %fusion = f32[1024]{0:T(1024)S(1)} fusion(bf16[1024,4608]{1,0:T(8,128)(2,1)} %all-gather.6.cloned.1.call-done), kind=kLoop, calls=%fused_computation.3 | loop fusion | flops 14154752 | bytes 9441280 | tf_op jit(solution)/shard_map/reduce_sum | solution.py:41
  89.7 0.0 copy-done.1
  89.7 0.6 copy-done
  90.3 26.1 %exponential_reduce_fusion = (f32[1024]{0:T(1024)S(1)}, f32[1024,2000]{0,1:T(8,128)}) fusion(bf16[2000,4608]{1,0:T(8,128)(2,1)} %param.9, bf16[1024,4608]{1,0:T(8,128)(2,1)S(1)} %copy-done, f32[4608]{0:T(1024)S(1)} %copy-done.1, f32[1024]{0:T(1024)S(1)} %add_rsqrt_fusion), kind=kOutput, calls=%fused_computation.9 | convolution fusion | flops 18899386368 | bytes 36087808 | tf_op jit(solution)/shard_map/dot_general | solution.py:61
  116.4 45.1 %gather_fusion = f32[1024]{0:T(1024)S(1)} fusion(f32[1024,2000]{0,1:T(8,128)} %get-tuple-element.46, s32[1024]{0:T(1024)S(1)} %bitcast.31), kind=kCustom, calls=%fused_computation | custom fusion | bytes 16384 | tf_op jit(solution)/shard_map/jit(take_along_axis)/gather | solution.py:69
  161.5 7.8 %all-reduce.5 = (f32[1024]{0:T(1024)S(1)}, f32[1024]{0:T(1024)S(1)}) all-reduce(f32[1024]{0:T(1024)S(1)} %select_select_fusion.1, f32[1024]{0:T(1024)S(1)} %get-tuple-element.45), channel_id=1, replica_groups=mesh['dp_0'=4,'dp_1'=2,'tensor_0'=4,'tensor_1'=4] {'dp_0'}, use_global_device_ids=true, to_apply=%region_1.2 | all-reduce | flops 2048 | bytes 16384 | tf_op jit(solution)/shard_map/psum | solution.py:35
  169.4 2.5 %all-reduce.7 = (f32[1024]{0:T(1024)S(1)}, f32[1024]{0:T(1024)S(1)}) all-reduce(f32[1024]{0:T(1024)S(1)} %get-tuple-element.18, f32[1024]{0:T(1024)S(1)} %get-tuple-element.19), channel_id=1, replica_groups=mesh['dp_0'=4,'dp_1'=2,'tensor_0'=4,'tensor_1'=4] {'dp_1'}, use_global_device_ids=true, to_apply=%region_2.3 | all-reduce | flops 2048 | bytes 16384 | tf_op jit(solution)/shard_map/psum | solution.py:35
  171.9 8.4 %all-reduce.3 = (f32[1024]{0:T(1024)S(1)}, f32[1024]{0:T(1024)S(1)}) all-reduce(f32[1024]{0:T(1024)S(1)} %get-tuple-element.23, f32[1024]{0:T(1024)S(1)} %get-tuple-element.24), channel_id=1, replica_groups=mesh['dp_0'=4,'dp_1'=2,'tensor_0'=4,'tensor_1'=4] {'tensor_0'}, use_global_device_ids=true, to_apply=%region_3.4 | all-reduce | flops 2048 | bytes 16384 | tf_op jit(solution)/shard_map/psum | solution.py:35
  180.3 10.1 %all-reduce.1 = (f32[1024]{0:T(1024)S(1)}, f32[1024]{0:T(1024)S(1)}) all-reduce(f32[1024]{0:T(1024)S(1)} %get-tuple-element.13, f32[1024]{0:T(1024)S(1)} %get-tuple-element.14), channel_id=1, replica_groups=mesh['dp_0'=4,'dp_1'=2,'tensor_0'=4,'tensor_1'=4] {'tensor_1'}, use_global_device_ids=true, to_apply=%region_4.5 | all-reduce | flops 2048 | bytes 16384 | tf_op jit(solution)/shard_map/psum | solution.py:35
  190.4 0.8 fusion.35
  191.2 0.6 reshape.259
  192.5 8.5 %all-reduce.4 = (f32[]{:T(128)}, f32[]{:T(128)}, f32[]{:T(128)}) all-reduce(f32[]{:T(128)S(6)} %neg.3, f32[]{:T(128)} %get-tuple-element.4, f32[]{:T(128)} %get-tuple-element.3), channel_id=1, replica_groups=mesh['dp_0'=4,'dp_1'=2,'tensor_0'=4,'tensor_1'=4] {'dp_0'}, use_global_device_ids=true, to_apply=%region_11.12 | all-reduce | flops 3 | bytes 24 | tf_op jit(solution)/shard_map/psum | solution.py:35
  201.0 3.1 %all-reduce.6 = (f32[]{:T(128)}, f32[]{:T(128)}, f32[]{:T(128)}) all-reduce(f32[]{:T(128)} %get-tuple-element.15, f32[]{:T(128)} %get-tuple-element.16, f32[]{:T(128)} %get-tuple-element.17), channel_id=1, replica_groups=mesh['dp_0'=4,'dp_1'=2,'tensor_0'=4,'tensor_1'=4] {'dp_1'}, use_global_device_ids=true, to_apply=%region_12.13 | all-reduce | flops 3 | bytes 24 | tf_op jit(solution)/shard_map/psum | solution.py:35
  204.1 10.3 %all-reduce.2 = (f32[]{:T(128)}, f32[]{:T(128)}, f32[]{:T(128)}) all-reduce(f32[]{:T(128)} %get-tuple-element.20, f32[]{:T(128)} %get-tuple-element.21, f32[]{:T(128)} %get-tuple-element.22), channel_id=1, replica_groups=mesh['dp_0'=4,'dp_1'=2,'tensor_0'=4,'tensor_1'=4] {'tensor_0'}, use_global_device_ids=true, to_apply=%region_13.14 | all-reduce | flops 3 | bytes 24 | tf_op jit(solution)/shard_map/psum | solution.py:35
  214.4 9.7 %all-reduce = (f32[]{:T(128)}, f32[]{:T(128)}, f32[]{:T(128)}) all-reduce(f32[]{:T(128)} %get-tuple-element.10, f32[]{:T(128)} %get-tuple-element.11, f32[]{:T(128)} %get-tuple-element.12), channel_id=1, replica_groups=mesh['dp_0'=4,'dp_1'=2,'tensor_0'=4,'tensor_1'=4] {'tensor_1'}, use_global_device_ids=true, to_apply=%region_14.15 | all-reduce | flops 3 | bytes 24 | tf_op jit(solution)/shard_map/psum | solution.py:35
  (11 shorter events, 0.1 us)
Async XLA Ops:
  7.2 82.6 %copy-start.1 = (f32[4608]{0:T(1024)S(1)}, f32[4608]{0:T(1024)}, u32[]{:S(2)}) copy-start(f32[4608]{0:T(1024)} %param.6) | copy-start | bytes 55300
  7.2 76.8 %all-gather.6.cloned.1.call-start = ((), (), s32[]{:S(2)}) async-start(), calls=%async_computation | async-start | bytes 9510912 | tf_op jit(solution)/shard_map/all_gather | solution.py:60
  84.0 6.4 %copy-start = (bf16[1024,4608]{1,0:T(8,128)(2,1)S(1)}, bf16[1024,4608]{1,0:T(8,128)(2,1)}, u32[]{:S(2)}) copy-start(bf16[1024,4608]{1,0:T(8,128)(2,1)} %all-gather.6.cloned.1.call-done) | copy-start | bytes 28311556
Sparse Core Ops, SparseCore 0:
  11.1 72.8 all-gather.5
where the time goes:
time: 237 us; the launch traced here: 236 us
  blocking collectives  96.5 us (41%)
  local copies, waits for them, and re-layouts  51.3 us (22%)
  matrix products  26.1 us (11%)
  waiting for transfers between devices  24.7 us (10%)
  between operations  19.7 us (8%)
  other arithmetic  17.3 us (7%)
    psum x8, blocking collectives, one_axis_at_a_time(): value = lax.psum(value, axis)  60.4 us
    gather x1, local copies, waits for them, and re-layouts, per_device(): jnp.take_along_axis(capped, jnp.clip(local, 0, vocab_dev - 1)[:, None], a...  45.1 us
    all_gather x4, blocking collectives, gather_in_order(): pieces = lax.all_gather(pieces, axes[k], axis=0, tiled=True)  36.2 us
    dot_general x1, matrix products, per_device(): lax.dot_general(rows, embed, (((1,), (1,)), ((), ())), preferred_element_...  26.1 us
    all_gather x1, waiting for transfers between devices, per_device(): rows = normalize(lax.all_gather(flat, DP_TENSOR, axis=0, tiled=True), gain)  24.7 us
    convert_element_type x1, other arithmetic, per_device(): live_all = (positions < jnp.take(lengths, batch_ids)).astype(jnp.float32)  5.82 us
    reduce_sum x1, other arithmetic, normalize(): meansq = jnp.mean(values * values, axis=-1, keepdims=True)  5.72 us
    gather x10, other arithmetic, per_device(): live_all = (positions < jnp.take(lengths, batch_ids)).astype(jnp.float32)  4.91 us
  transfers between devices with their start and end apart: 1, of which 1 were waited for; matrix products, arithmetic and copies ran while one was open for 6% of the time, Pallas kernels for 0%

commit v1 on v0

--- a/solution.py
+++ b/solution.py
@@ -32,7 +32,8 @@
 
 def one_axis_at_a_time(value, axes):
     for axis in axes:
-        value = lax.psum(value, axis)
+        parts = lax.all_gather(value, axis, axis=0, tiled=False)
+        value = parts.sum(axis=0)
     return value
 
 

time: 237 us -> 305 us (1.29)
  blocking collectives: 96.5 us -> 139 us
  local copies, waits for them, and re-layouts: 51.3 us -> 70.5 us
  other arithmetic: 17.3 us -> 24.6 us
    all_gather x0 -> x8, blocking collectives: none -> 75.7 us  [one_axis_at_a_time(): parts = lax.all_gather(value, axis, axis=0, tiled=False)]
    psum x8 -> x0, blocking collectives: 60.4 us -> none  [one_axis_at_a_time(): value = lax.psum(value, axis)]
    unnamed x0 -> x4, blocking collectives: none -> 26.7 us
    unnamed x8 -> x42, local copies, waits for them, and re-layouts: 1.54 us -> 20.7 us
    reduce_sum x0 -> x20, other arithmetic: none -> 7.43 us  [one_axis_at_a_time(): value = parts.sum(axis=0)]
  transfers between devices with their start and end apart: 1 -> 1, of which waited for: 1 -> 1; matrix products, arithmetic and copies ran while one was open for 6% -> 5% of each run, Pallas kernels for 0% -> 0%
where the time goes in v1:
time: 305 us; the launch traced here: 303 us
  blocking collectives  139 us (46%)
  local copies, waits for them, and re-layouts  70.5 us (23%)
  matrix products  26.1 us (9%)
  other arithmetic  24.6 us (8%)
  waiting for transfers between devices  23.5 us (8%)
  between operations  19.9 us (7%)
    all_gather x8, blocking collectives, one_axis_at_a_time(): parts = lax.all_gather(value, axis, axis=0, tiled=False)  75.7 us
    gather x1, local copies, waits for them, and re-layouts, per_device(): jnp.take_along_axis(capped, jnp.clip(local, 0, vocab_dev - 1)[:, None], a...  45.1 us
    all_gather x4, blocking collectives, gather_in_order(): pieces = lax.all_gather(pieces, axes[k], axis=0, tiled=True)  36.2 us
    unnamed x4, blocking collectives  26.7 us
    dot_general x1, matrix products, per_device(): lax.dot_general(rows, embed, (((1,), (1,)), ((), ())), preferred_element_...  26.1 us
    all_gather x1, waiting for transfers between devices, per_device(): rows = normalize(lax.all_gather(flat, DP_TENSOR, axis=0, tiled=True), gain)  23.5 us
    unnamed x42, local copies, waits for them, and re-layouts  20.7 us
    reduce_sum x20, other arithmetic, one_axis_at_a_time(): value = parts.sum(axis=0)  7.43 us
  transfers between devices with their start and end apart: 1, of which 1 were waited for; matrix products, arithmetic and copies ran while one was open for 5% of the time, Pallas kernels for 0%

profile of v1, /device:TPU:0, one launch (start us, length us, event | category | flops | bytes accessed | tf_op | source)
XLA Modules:
  0.0 303.4 jit_solution(15006843411572801947)
XLA Ops:
  7.2 1.5 reshape.313
  8.8 0.8 reshape.428
  9.5 9.8 %all-gather.7 = s32[4,1,8]{2,1,0:T(1,128)S(1)} all-gather(s32[1,1,8]{2,1,0:T(1,128)S(1)} %reshape.428), channel_id=1, replica_groups=mesh['dp_0'=4,'dp_1'=2,'tensor_0'=4,'tensor_1'=4] {'dp_0'}, dimensions={0}, use_global_device_ids=true | all-gather | bytes 160 | tf_op jit(solution)/shard_map/all_gather | solution.py:22
  19.4 11.3 %all-gather.8 = s32[4,4,8]{2,1,0:T(4,128)S(1)} all-gather(s32[1,4,8]{2,1,0:T(4,128)S(1)} %bitcast.56), channel_id=1, replica_groups=mesh['dp_0'=4,'dp_1'=2,'tensor_0'=4,'tensor_1'=4] {'tensor_0'}, dimensions={0}, use_global_device_ids=true | all-gather | bytes 640 | tf_op jit(solution)/shard_map/all_gather | solution.py:22
  30.8 13.2 %all-gather.9 = s32[4,16,8]{1,2,0:T(8,128)S(1)} all-gather(s32[1,16,8]{1,2,0:T(8,128)S(1)} %copy.28), channel_id=1, replica_groups=mesh['dp_0'=4,'dp_1'=2,'tensor_0'=4,'tensor_1'=4] {'tensor_1'}, dimensions={0}, use_global_device_ids=true | all-gather | bytes 2560 | tf_op jit(solution)/shard_map/all_gather | solution.py:22
  44.1 1.8 all-gather.10
  46.5 1.3 dynamic-slice
  48.3 1.9 fusion.39
  50.2 4.5 %compare_select_fusion.3 = s32[1024,1]{0,1:T(1,128)S(1)} fusion(s32[]{:T(128)} %bitcast.9, s32[]{:T(128)} %bitcast.10, s32[]{:T(128)} %bitcast.11, s32[]{:T(128)} %bitcast.12, s32[]{:T(128)} %bitcast.13, s32[]{:T(128)} %bitcast.15, s32[]{:T(128)} %bitcast.14), kind=kLoop, calls=%fused_computation.23 | loop fusion | flops 60416 | bytes 4124 | tf_op jit(solution)/shard_map/jit(_take)/gather | solution.py:59
  54.8 5.7 %fusion.36 = f32[1024]{0:T(1024)S(1)} fusion(pred[1024]{0:T(1024)(128)(4,1)S(1)} %compare_reduce_fusion, pred[1024]{0:T(1024)(128)(4,1)S(1)} %compare_reduce_fusion.1, pred[1024]{0:T(1024)(128)(4,1)S(1)} %compare_reduce_fusion.2, pred[1024]{0:T(1024)(128)(4,1)S(1)} %compare_reduce_fusion.3, pred[1024]{0:T(1024)(128)(4,1)S(1)} %compare_reduce_fusion.4, ...), kind=kLoop, calls=%fused_computation.92 | loop fusion | flops 73728 | bytes 17444 | tf_op jit(solution)/shard_map/convert_element_type | solution.py:59
  60.5 23.5 %all-gather.14.cloned.1.call-done = bf16[1024,4608]{1,0:T(8,128)(2,1)} async-done(((bf16[8,4608]{1,0:T(8,128)(2,1)}), bf16[1024,4608]{1,0:T(8,128)(2,1)}) %all-gather.14.cloned.1.call-update) | async-done | bytes 9437200 | tf_op jit(solution)/shard_map/all_gather | solution.py:61
  84.0 5.7 %fusion = f32[1024]{0:T(1024)S(1)} fusion(bf16[1024,4608]{1,0:T(8,128)(2,1)} %all-gather.14.cloned.1.call-done), kind=kLoop, calls=%fused_computation.3 | loop fusion | flops 14154752 | bytes 9441280 | tf_op jit(solution)/shard_map/reduce_sum | solution.py:42
  89.7 0.6 copy-done
  90.4 26.1 %exponential_reduce_fusion = (f32[1024]{0:T(1024)S(1)}, f32[1024,2000]{0,1:T(8,128)}) fusion(bf16[2000,4608]{1,0:T(8,128)(2,1)} %param.9, bf16[1024,4608]{1,0:T(8,128)(2,1)S(1)} %copy-done, f32[4608]{0:T(1024)S(1)} %copy-done.1, f32[1024]{0:T(1024)S(1)} %add_rsqrt_fusion), kind=kOutput, calls=%fused_computation.9 | convolution fusion | flops 18899386368 | bytes 36087808 | tf_op jit(solution)/shard_map/dot_general | solution.py:62
  116.5 12.0 %all-gather.3 = f32[4096]{0:T(1024)S(1)} all-gather(f32[1024]{0:T(1024)S(1)} %get-tuple-element.37), channel_id=5, replica_groups=mesh['dp_0'=4,'dp_1'=2,'tensor_0'=4,'tensor_1'=4] {'dp_0'}, dimensions={0}, use_global_device_ids=true | all-gather | bytes 20480 | tf_op jit(solution)/shard_map/all_gather | solution.py:35
  128.5 1.8 all-gather.4
  130.4 12.0 %all-gather.5 = f32[4096]{0:T(1024)S(1)} all-gather(f32[1024]{0:T(1024)S(1)} %reduce_sum.232), channel_id=7, replica_groups=mesh['dp_0'=4,'dp_1'=2,'tensor_0'=4,'tensor_1'=4] {'tensor_0'}, dimensions={0}, use_global_device_ids=true | all-gather | bytes 20480 | tf_op jit(solution)/shard_map/all_gather | solution.py:35
  142.4 12.0 %all-gather.6 = f32[4096]{0:T(1024)S(1)} all-gather(f32[1024]{0:T(1024)S(1)} %reduce_sum.233), channel_id=8, replica_groups=mesh['dp_0'=4,'dp_1'=2,'tensor_0'=4,'tensor_1'=4] {'tensor_1'}, dimensions={0}, use_global_device_ids=true | all-gather | bytes 20480 | tf_op jit(solution)/shard_map/all_gather | solution.py:35
  154.5 45.1 %gather_fusion = f32[1024]{0:T(1024)S(1)} fusion(f32[1024,2000]{0,1:T(8,128)} %get-tuple-element.38, s32[1024]{0:T(1024)S(1)} %bitcast.50), kind=kCustom, calls=%fused_computation | custom fusion | bytes 16384 | tf_op jit(solution)/shard_map/jit(take_along_axis)/gather | solution.py:70
  199.6 12.0 %all-gather.11 = f32[4,1,1024]{2,1,0:T(1,128)S(1)} all-gather(f32[1,1,1024]{2,1,0:T(1,128)S(1)} %fusion.35), channel_id=1, replica_groups=mesh['dp_0'=4,'dp_1'=2,'tensor_0'=4,'tensor_1'=4] {'dp_0'}, dimensions={0}, use_global_device_ids=true | all-gather | bytes 20480 | tf_op jit(solution)/shard_map/all_gather | solution.py:35
  211.6 1.8 all-gather
  213.5 12.0 %all-gather.1 = f32[4096]{0:T(1024)S(1)} all-gather(f32[1024]{0:T(1024)S(1)} %reduce_sum.227), channel_id=3, replica_groups=mesh['dp_0'=4,'dp_1'=2,'tensor_0'=4,'tensor_1'=4] {'tensor_0'}, dimensions={0}, use_global_device_ids=true | all-gather | bytes 20480 | tf_op jit(solution)/shard_map/all_gather | solution.py:35
  225.5 12.0 %all-gather.2 = f32[4096]{0:T(1024)S(1)} all-gather(f32[1024]{0:T(1024)S(1)} %reduce_sum.228), channel_id=4, replica_groups=mesh['dp_0'=4,'dp_1'=2,'tensor_0'=4,'tensor_1'=4] {'tensor_1'}, dimensions={0}, use_global_device_ids=true | all-gather | bytes 20480 | tf_op jit(solution)/shard_map/all_gather | solution.py:35
  237.6 0.7 fusion.37
  239.0 0.7 dynamic-update-slice
  239.7 1.4 dynamic-update-slice.4
  241.1 1.4 dynamic-update-slice.8
  243.0 7.7 %all-reduce.14 = (f32[4]{0:T(128)S(1)}, f32[4]{0:T(128)S(1)}, f32[4]{0:T(128)S(1)}) all-reduce(f32[4]{0:T(128)S(1)} %dynamic-update-slice, f32[4]{0:T(128)S(1)} %dynamic-update-slice.4, f32[4]{0:T(128)S(1)} %dynamic-update-slice.8), channel_id=1, replica_groups=mesh['dp_0'=4,'dp_1'=2,'tensor_0'=4,'tensor_1'=4] {'dp_0'}, use_global_device_ids=true, to_apply=%add | all-reduce | flops 12 | bytes 96
  250.8 0.6 reduce_sum.236
  252.0 1.4 dynamic-update-slice.1
  253.4 1.4 dynamic-update-slice.5
  254.8 0.6 reduce_sum.246
  255.4 1.4 dynamic-update-slice.9
  257.4 2.4 all-reduce.15
  259.8 0.6 reduce_sum.237
  261.0 1.4 dynamic-update-slice.2
  262.4 1.4 dynamic-update-slice.6
  264.4 1.4 dynamic-update-slice.10
  266.4 7.7 %all-reduce.13 = (f32[4]{0:T(128)S(1)}, f32[4]{0:T(128)S(1)}, f32[4]{0:T(128)S(1)}) all-reduce(f32[4]{0:T(128)S(1)} %dynamic-update-slice.2, f32[4]{0:T(128)S(1)} %dynamic-update-slice.6, f32[4]{0:T(128)S(1)} %dynamic-update-slice.10), channel_id=1, replica_groups=mesh['dp_0'=4,'dp_1'=2,'tensor_0'=4,'tensor_1'=4] {'tensor_0'}, use_global_device_ids=true, to_apply=%add.2 | all-reduce | flops 12 | bytes 96
  274.1 0.6 reduce_sum.238
  275.3 1.4 dynamic-update-slice.3
  276.7 1.4 dynamic-update-slice.7
  278.7 1.4 dynamic-update-slice.11
  280.1 0.6 reshape.314
  280.8 8.9 %all-reduce.12 = (f32[4]{0:T(128)S(1)}, f32[4]{0:T(128)S(1)}, f32[4]{0:T(128)S(1)}) all-reduce(f32[4]{0:T(128)S(1)} %dynamic-update-slice.3, f32[4]{0:T(128)S(1)} %dynamic-update-slice.7, f32[4]{0:T(128)S(1)} %dynamic-update-slice.11), channel_id=1, replica_groups=mesh['dp_0'=4,'dp_1'=2,'tensor_0'=4,'tensor_1'=4] {'tensor_1'}, use_global_device_ids=true, to_apply=%add.3 | all-reduce | flops 12 | bytes 96
  289.6 0.6 reduce_sum.239
  290.2 0.7 reduce_sum.244
  292.3 0.6 reduce_sum.249
  (73 shorter events, 6.4 us)
Async XLA Ops:
  7.2 82.6 %copy-start.1 = (f32[4608]{0:T(1024)S(1)}, f32[4608]{0:T(1024)}, u32[]{:S(2)}) copy-start(f32[4608]{0:T(1024)} %param.6) | copy-start | bytes 55300
  7.2 76.8 %all-gather.14.cloned.1.call-start = ((), (), s32[]{:S(2)}) async-start(), calls=%async_computation | async-start | bytes 9510912 | tf_op jit(solution)/shard_map/all_gather | solution.py:61
  84.0 6.4 %copy-start = (bf16[1024,4608]{1,0:T(8,128)(2,1)S(1)}, bf16[1024,4608]{1,0:T(8,128)(2,1)}, u32[]{:S(2)}) copy-start(bf16[1024,4608]{1,0:T(8,128)(2,1)} %all-gather.14.cloned.1.call-done) | copy-start | bytes 28311556
  90.3 152.1 %copy-start.4 = (u32[128]{0:T(128)S(1)}, u32[128]{0:T(128)}, u32[]{:S(2)}) copy-start(u32[128]{0:T(128)} %constant.184) | copy-start | bytes 1540
  90.3 166.4 %copy-start.3 = (u32[128]{0:T(128)S(1)}, u32[128]{0:T(128)}, u32[]{:S(2)}) copy-start(u32[128]{0:T(128)} %constant.189) | copy-start | bytes 1540
  90.4 175.5 %copy-start.2 = (u32[128]{0:T(128)S(1)}, u32[128]{0:T(128)}, u32[]{:S(2)}) copy-start(u32[128]{0:T(128)} %constant.194) | copy-start | bytes 1540
Sparse Core Ops, SparseCore 0:
  11.1 72.8 all-gather.13
